TPU v7x, 512 devices: a whole 4x8x8 slice. The times are simulated.
512 devices in a mesh: group: 16 (over y, core), page: 8 (over z), tensor: 4 (over x).
Axes of the slice: x: 4, y: 8, z: 8, core: 2. Of those that a mesh axis runs over, the one named last changes fastest.
Arguments:
- query: bfloat16 [32, 8192], P(None, 'tensor'), may hold values from -400 to 400
- cache_keys: bfloat16 [16384, 16, 1024], P(('group', 'page'), None, 'tensor'), may hold values from -6 to 6
- cache_values: bfloat16 [16384, 16, 1024], P(('group', 'page'), None, 'tensor'), may hold values from -6 to 6
- new_keys: bfloat16 [2048, 16, 1024], P(('group', 'page'), None, 'tensor'), may hold values from -6 to 6
- new_values: bfloat16 [2048, 16, 1024], P(('group', 'page'), None, 'tensor'), may hold values from -6 to 6
- page_map: int32 [2048, 2], replicated, may hold values from 0 to 127, as said below
- page_table: int32 [32, 2048], replicated, may hold values from 0 to 16383, as said below
- lengths: int32 [32], replicated, may hold values from 1009 to 32768, as said below
- out_weight: bfloat16 [8192, 8192], P('tensor', ('group', 'page')), may hold values from -0.0625 to 0.0625
Outputs:
- result: bfloat16 [32, 8192], P(None, ('group', 'page', 'tensor'))
Inputs may be any that keep to these rules, and one draw needn't show every extreme that they name: `page_map`: new page r lies on the device of group index r // 128 and page index (r // 16) mod 8; column 0 names the group index of the receiving device at the same page index, column 1 the slot of its cache shard that the page replaces. Of one device's 16 new pages at most 2 go to one receiver, and at every page index one receiver gets exactly 2 from every sender; the slots that one receiver gets are distinct. `page_table`: entry j of row s is the global slot (group index * 8 + page index) * 128 + slot of the j-th page of sequence s. The first ceil(lengths[s] / 16) entries of a row are live; live entries are distinct over all sequences and include every slot named by the page map; the other entries are arbitrary. `lengths`: one sequence has exactly 32768 tokens.
All inputs are finite; a program needn't handle non-finite values.
Results may differ from a plain program's by a relative error of at most 0.0065.
Values may be sent and summed in bfloat16 or wider, within the bound.
A program may use at most 64 MiB of HBM per device.

v0:
```python
import jax
import jax.numpy as jnp
from jax import lax
from jax.sharding import Mesh
from jax.sharding import PartitionSpec as P

HD = 128
PAGE = 16
GROUP = ("group_0", "group_1")
GROUP_PAGE = ("group_0", "group_1", "page")
GROUP_PAGE_TENSOR = ("group_0", "group_1", "page", "tensor")


very_low = -1e30


def side_by_side(arrays, axis, split_dim, concat_dim, along):
    widths = [a.shape[along] for a in arrays]
    both = jnp.concatenate(arrays, axis=along)
    out = lax.all_to_all(both, axis, split_axis=split_dim, concat_axis=concat_dim, tiled=True)
    return tuple(jnp.split(out, [sum(widths[:k]) for k in range(1, len(widths))], axis=along))


def collected_together(shard, axis):
    leaves = jax.tree.leaves(shard)
    sequence = sorted(range(len(leaves)), key=lambda k: -leaves[k].size)
    width = (1, *leaves[sequence[0]].shape)[-1]
    lines = [
        jnp.pad(leaves[k].reshape(-1), (0, -leaves[k].size % width)).reshape(-1, width)
        for k in sequence
    ]
    both, at, found = (lax.all_gather(jnp.concatenate(lines), axis), 0, {})
    for k, line in zip(sequence, lines):
        slab = both[:, at : at + len(line)].reshape(len(both), -1)
        found[k] = slab[:, : leaves[k].size].reshape(-1, *leaves[k].shape)
        at += len(line)
    numbers = iter(range(len(leaves)))
    return jax.tree.map(lambda _: found[next(numbers)], shard)


def joined_all(shard, axes, combine):
    for axis in axes:
        pieces = collected_together(shard, axis)
        shard = jax.tree.map(lambda part: part[0], pieces)
        for k in range(1, lax.axis_size(axis)):
            shard = combine(shard, jax.tree.map(lambda part: part[k], pieces))
    return shard


def split_up(shard, dim, count):
    shape = shard.shape
    blocks = shard.reshape(*shape[:dim], count, shape[dim] // count, *shape[dim + 1 :])
    return jnp.moveaxis(blocks, dim, 0)


def summed_on_arrival(shard, axis, dim):
    count = lax.axis_size(axis)
    blocks = lax.all_to_all(split_up(shard, dim, count), axis, 0, 0, tiled=True)
    return jnp.sum(blocks, axis=0)


def combine(first, second):
    highest = jnp.maximum(first[0], second[0])
    first_scale = jnp.exp(first[0] - highest)
    second_scale = jnp.exp(second[0] - highest)
    total = first[1] * first_scale + second[1] * second_scale
    row_count = highest.shape[0]
    head_count = highest.shape[1]
    mixed = first[2].reshape(row_count, head_count, -1) * first_scale[..., None]
    mixed = mixed + second[2].reshape(row_count, head_count, -1) * second_scale[..., None]
    return (highest, total, mixed.reshape(row_count, -1))


def place_pages(destination, count, pages):
    picker = (destination[None, :] == jnp.arange(count, dtype=jnp.int32)[:, None]).astype(
        pages.dtype
    )
    flat = pages.reshape(pages.shape[0], -1)
    placed = jnp.dot(picker, flat, preferred_element_type=jnp.float32).astype(pages.dtype)
    return placed.reshape((count,) + pages.shape[1:])


def on_device(
    query, cache_keys, cache_values, new_keys, new_values, page_map, page_table, lengths, out_weight
):
    groups = lax.axis_size(GROUP)
    page_count = lax.axis_size("page")
    group_index = lax.axis_index(GROUP)
    page_index = lax.axis_index("page")
    slot_count = cache_keys.shape[0]
    width = cache_keys.shape[2]
    fresh_count = new_keys.shape[0]
    capacity = max(1, 2 * fresh_count // groups)
    sheet = page_map.reshape(groups, page_count, fresh_count, 2)
    mine = lax.dynamic_index_in_dim(sheet, page_index, axis=1, keepdims=False)
    targets = mine[:, :, 0]
    target_slots = mine[:, :, 1]
    receiver_hits = (
        targets[:, :, None] == jnp.arange(groups, dtype=jnp.int32)[None, None, :]
    ).astype(jnp.int32)
    position = jnp.sum((jnp.cumsum(receiver_hits, axis=1) - receiver_hits) * receiver_hits, axis=2)
    arriving = targets == group_index
    own_targets = lax.dynamic_index_in_dim(targets, group_index, axis=0, keepdims=False)
    own_position = lax.dynamic_index_in_dim(position, group_index, axis=0, keepdims=False)
    outbox_slot = own_targets * capacity + own_position
    outbox_keys = place_pages(outbox_slot, groups * capacity, new_keys)
    outbox_values = place_pages(outbox_slot, groups * capacity, new_values)
    outbox_keys = outbox_keys.reshape((groups, capacity) + new_keys.shape[1:])
    outbox_values = outbox_values.reshape((groups, capacity) + new_values.shape[1:])
    got_keys, got_values = side_by_side((outbox_keys, outbox_values), GROUP, 0, 0, 1)
    inbox_slot = jnp.arange(groups, dtype=jnp.int32)[:, None] * capacity + position
    box_ids = jnp.arange(groups * capacity, dtype=jnp.int32)
    box_match = (inbox_slot.reshape(-1)[None, :] == box_ids[:, None]) & arriving.reshape(-1)[
        None, :
    ]
    placed = jnp.sum(jnp.where(box_match, target_slots.reshape(-1)[None, :] + 1, 0), axis=1) - 1
    placed = jnp.where(placed < 0, slot_count, placed)
    arrived_keys = got_keys.reshape((groups * capacity,) + new_keys.shape[1:])
    arrived_values = got_values.reshape((groups * capacity,) + new_values.shape[1:])
    fresh_hit = jnp.any(placed[None, :] == jnp.arange(slot_count, dtype=jnp.int32)[:, None], axis=1)
    key_cache = jnp.where(
        fresh_hit[:, None, None], place_pages(placed, slot_count, arrived_keys), cache_keys
    )
    value_cache = jnp.where(
        fresh_hit[:, None, None], place_pages(placed, slot_count, arrived_values), cache_values
    )
    shard_number = group_index * page_count + page_index
    slot_base = shard_number * slot_count
    seq_count = page_table.shape[0]
    page_limit = page_table.shape[1]
    page_numbers = jnp.arange(page_limit, dtype=jnp.int32)[None, :]
    used_pages = (lengths + PAGE - 1) // PAGE
    local_slot = page_table - slot_base
    live = (page_numbers < used_pages[:, None]) & (local_slot >= 0) & (local_slot < slot_count)
    local_slot = jnp.where(live, local_slot, slot_count)
    token_fill = jnp.clip(lengths[:, None] - page_numbers * PAGE, 0, PAGE)
    block = min(page_limit, 256)
    slot_ids = jnp.arange(slot_count, dtype=jnp.int32)[None, None, :]
    member = jnp.zeros((seq_count, slot_count), jnp.bool_)
    filled = jnp.zeros((slot_count,), jnp.int32)
    for start in range(0, page_limit, block):
        match = local_slot[:, start : start + block, None] == slot_ids
        member = member | jnp.any(match, axis=1)
        filled = filled + jnp.sum(
            jnp.where(match, token_fill[:, start : start + block, None], 0), axis=(0, 1)
        )
    kv_heads = width // HD
    share = query.shape[1] // HD // kv_heads
    picker = member.astype(jnp.bfloat16)
    query_slots = lax.dot_general(
        picker, query, (((0,), (0,)), ((), ())), preferred_element_type=jnp.float32
    )
    query_slots = query_slots.astype(jnp.bfloat16).reshape(slot_count, kv_heads, share, HD)
    key_blocks = key_cache.reshape(slot_count, PAGE, kv_heads, HD)
    value_blocks = value_cache.reshape(slot_count, PAGE, kv_heads, HD)
    scores = jnp.einsum(
        "skgd,stkd->skgt", query_slots, key_blocks, preferred_element_type=jnp.float32
    ) * HD ** (-0.5)
    visible = (jnp.arange(PAGE, dtype=jnp.int32)[None, :] < filled[:, None])[:, None, None, :]
    scores = jnp.where(visible, scores, very_low)
    slot_high = jnp.max(scores, axis=3)
    seq_high = jnp.max(jnp.where(member[:, :, None, None], slot_high[None], very_low), axis=1)
    anchor_high = jnp.max(jnp.where(member[:, :, None, None], seq_high[:, None], very_low), axis=0)
    raw_weights = jnp.where(visible, jnp.exp(scores - anchor_high[..., None]), 0.0)
    weight_sum = jnp.sum(raw_weights, axis=3)
    partial_value = jnp.einsum(
        "skgt,stkd->skgd",
        raw_weights.astype(jnp.bfloat16),
        value_blocks,
        preferred_element_type=jnp.float32,
    )
    selector = member.astype(jnp.float32)
    summed = jnp.dot(selector, partial_value.reshape(slot_count, -1))
    total = jnp.dot(selector, weight_sum.reshape(slot_count, -1))
    highest = seq_high.reshape(seq_count, -1)
    head_count = highest.shape[1]
    pieces = joined_all((highest, total, summed), GROUP_PAGE, combine)
    attention = pieces[2].reshape(seq_count, head_count, HD) / pieces[1][..., None]
    attention = attention.reshape(seq_count, -1).astype(jnp.bfloat16)
    partial_terms = jnp.dot(attention, out_weight, preferred_element_type=jnp.float32)
    return summed_on_arrival(partial_terms, "tensor", 1).astype(jnp.bfloat16)


def solution(mesh):
    finer = Mesh(
        mesh.devices.reshape(8, 2, mesh.shape["page"], mesh.shape["tensor"]),
        ("group_0", "group_1", "page", "tensor"),
    )
    placed = (
        P(None, "tensor"),
        P(GROUP_PAGE, None, "tensor"),
        P(GROUP_PAGE, None, "tensor"),
        P(GROUP_PAGE, None, "tensor"),
        P(GROUP_PAGE, None, "tensor"),
        P(),
        P(),
        P(),
        P("tensor", GROUP_PAGE),
    )
    return jax.shard_map(
        on_device,
        mesh=finer,
        in_specs=placed,
        out_specs=P(None, GROUP_PAGE_TENSOR),
        check_vma=False,
    )
```

profile of v0, /device:TPU:8, one launch (start us, length us, event | category | flops | bytes accessed | tf_op | source)
XLA Modules:
  0.0 189.7 jit_solution(1042898388656342192)
XLA Ops:
  6.5 0.9 reshape.1159
  7.6 0.5 fusion.82
  8.1 1.0 copy.65
  9.1 0.2 add_reduce_fusion
  9.3 0.2 convolution_convert_fusion.2
  9.6 0.9 copy.63
  10.5 0.2 convolution_convert_fusion.3
  10.8 0.8 pad_maximum_fusion
  11.6 9.2 %all-to-all-start = ((bf16[16,4,16,256]{3,2,1,0:T(8,128)(2,1)}), bf16[16,4,16,256]{3,2,1,0:T(8,128)(2,1)S(1)}, u32[]{:S(2)}, u32[]{:S(2)}) async-start(bf16[16,4,16,256]{3,2,1,0:T(8,128)(2,1)} %pad_maximum_fusion), calls=%async_computation | async-start | bytes 1048576 | tf_op jit(solution)/shard_map/all_to_all | solution.py:20
  21.5 1.4 fusion
  23.0 1.4 fusion.1
  24.4 1.4 fusion.2
  25.8 1.4 fusion.3
  27.2 1.4 fusion.4
  28.6 1.4 fusion.5
  30.0 1.4 fusion.7
  31.4 1.4 fusion.6
  32.9 0.3 fusion.9
  33.5 2.8 %select_reduce_fusion = s32[128]{0:T(128)S(1)} fusion(s32[32,256]{1,0:T(8,128)S(1)} %get-tuple-element.82, s32[32,256]{1,0:T(8,128)S(1)} %get-tuple-element.90), kind=kLoop, calls=%fused_computation.4 | loop fusion | flops 3145600 | bytes 66048 | tf_op jit(solution)/shard_map/reduce_sum | solution.py:144
  36.3 2.8 %select_reduce_fusion.1 = s32[128]{0:T(128)S(1)} fusion(s32[32,256]{1,0:T(8,128)S(1)} %get-tuple-element.83, s32[32,256]{1,0:T(8,128)S(1)} %get-tuple-element.91), kind=kLoop, calls=%fused_computation.5 | loop fusion | flops 3145600 | bytes 66048 | tf_op jit(solution)/shard_map/reduce_sum | solution.py:144
  39.1 2.8 %select_reduce_fusion.2 = s32[128]{0:T(128)S(1)} fusion(s32[32,256]{1,0:T(8,128)S(1)} %get-tuple-element.84, s32[32,256]{1,0:T(8,128)S(1)} %get-tuple-element.92), kind=kLoop, calls=%fused_computation.6 | loop fusion | flops 3145600 | bytes 66048 | tf_op jit(solution)/shard_map/reduce_sum | solution.py:144
  41.9 2.8 %select_reduce_fusion.3 = s32[128]{0:T(128)S(1)} fusion(s32[32,256]{1,0:T(8,128)S(1)} %get-tuple-element.85, s32[32,256]{1,0:T(8,128)S(1)} %get-tuple-element.93), kind=kLoop, calls=%fused_computation.7 | loop fusion | flops 3145600 | bytes 66048 | tf_op jit(solution)/shard_map/reduce_sum | solution.py:144
  44.7 2.8 %select_reduce_fusion.4 = s32[128]{0:T(128)S(1)} fusion(s32[32,256]{1,0:T(8,128)S(1)} %get-tuple-element.86, s32[32,256]{1,0:T(8,128)S(1)} %get-tuple-element.94), kind=kLoop, calls=%fused_computation.8 | loop fusion | flops 3145600 | bytes 66048 | tf_op jit(solution)/shard_map/reduce_sum | solution.py:144
  47.5 2.8 %select_reduce_fusion.5 = s32[128]{0:T(128)S(1)} fusion(s32[32,256]{1,0:T(8,128)S(1)} %get-tuple-element.87, s32[32,256]{1,0:T(8,128)S(1)} %get-tuple-element.95), kind=kLoop, calls=%fused_computation.9 | loop fusion | flops 3145600 | bytes 66048 | tf_op jit(solution)/shard_map/reduce_sum | solution.py:144
  50.4 2.8 %select_reduce_fusion.7 = s32[128]{0:T(128)S(1)} fusion(s32[32,256]{1,0:T(8,128)S(1)} %get-tuple-element.88, s32[32,256]{1,0:T(8,128)S(1)} %get-tuple-element.96), kind=kLoop, calls=%fused_computation.11 | loop fusion | flops 3145600 | bytes 66048 | tf_op jit(solution)/shard_map/reduce_sum | solution.py:144
  53.2 2.8 %select_reduce_fusion.6 = s32[128]{0:T(128)S(1)} fusion(s32[32,256]{1,0:T(8,128)S(1)} %get-tuple-element.81, s32[32,256]{1,0:T(8,128)S(1)} %get-tuple-element.89), kind=kLoop, calls=%fused_computation.10 | loop fusion | flops 3145600 | bytes 66048 | tf_op jit(solution)/shard_map/reduce_sum | solution.py:144
  56.3 0.5 convolution_convert_fusion
  56.8 0.2 copy.70
  57.2 0.5 convolution_convert_fusion.1
  57.7 0.2 copy.68
  58.0 0.3 copy-done.3
  58.4 0.6 bitcast_select_fusion
  58.9 0.9 fusion.83
  59.9 0.2 select_reduce_fusion.9
  60.1 0.1 select_reduce_fusion.8
  60.4 0.1 copy.49
  60.5 0.8 fusion.19
  61.7 0.5 fusion.14
  62.2 0.2 fusion.11
  62.4 0.8 maximum_bitcast_fusion
  63.2 0.2 all-gather.11.cloned.1.call-start
  63.4 47.1 %all-gather.9.cloned.1.call-done = f32[8,34,2048]{2,1,0:T(8,128)} async-done(((f32[1,34,2048]{2,1,0:T(8,128)}), f32[8,34,2048]{2,1,0:T(8,128)}) %all-gather.9.cloned.1.call-update) | async-done | bytes 2228240 | tf_op jit(solution)/shard_map/all_gather | solution.py:32
  110.5 1.3 fusion.75
  112.9 0.1 mul.659
  113.0 0.1 mul.656
  113.2 0.1 mul.653
  113.3 0.1 mul.650
  113.4 0.1 mul.647
  113.6 0.1 mul.644
  113.7 0.1 mul.641
  114.5 0.1 mul.623
  114.6 1.8 fusion.41
  116.5 2.3 %all-gather.4 = f32[2,34,2048]{2,1,0:T(8,128)S(1)} all-gather(f32[1,34,2048]{2,1,0:T(8,128)S(1)} %maximum_bitcast_fusion.1), channel_id=3, replica_groups=mesh['group_0'=8,'group_1'=2,'page'=8,'tensor'=4] {'group_1'}, dimensions={0}, use_global_device_ids=true | all-gather | bytes 835584 | tf_op jit(solution)/shard_map/all_gather | solution.py:32
  119.4 0.2 fusion.40
  119.6 0.8 maximum_bitcast_fusion.2
  120.4 44.5 %all-gather.11.cloned.1.call-done = f32[8,34,2048]{2,1,0:T(8,128)} async-done(((f32[1,34,2048]{2,1,0:T(8,128)}), f32[8,34,2048]{2,1,0:T(8,128)}) %all-gather.11.cloned.1.call-update) | async-done | bytes 2228240 | tf_op jit(solution)/shard_map/all_gather | solution.py:32
  164.8 1.6 slice_bitcast_fusion.7
  166.9 1.3 fusion.74
  169.8 1.4 fusion.27
  171.3 0.2 fusion.84
  171.6 9.4 %all_to_all.10 = f32[4,1,512]{2,1,0:T(1,128)S(1)} all-to-all(f32[4,1,512]{2,1,0:T(1,128)S(1)} %reshape.1336), channel_id=1, replica_groups=mesh['group_0'=8,'group_1'=2,'page'=8,'tensor'=4] {'tensor'}, dimensions={0} | all-to-all | bytes 16384 | tf_op jit(solution)/shard_map/all_to_all | solution.py:58
  180.9 0.5 broadcast.283
  181.5 0.7 reduce.112
  182.2 0.6 bitcast_reduce_fusion
  (127 shorter events, 6.6 us)
Async XLA Ops:
  6.5 164.7 %copy-start = (bf16[2048,64]{0,1:T(8,128)(2,1)S(1)}, bf16[2048,64]{0,1:T(8,128)(2,1)}, u32[]{:S(2)}) copy-start(bf16[2048,64]{0,1:T(8,128)(2,1)} %param.17) | copy-start | bytes 786436
  6.5 14.8 %copy-start.6 = (s32[32]{0:T(128)S(1)}, s32[32]{0:T(128)}, u32[]{:S(2)}) copy-start(s32[32]{0:T(128)} %param.16) | copy-start | bytes 388
  6.5 14.8 %copy-start.4 = (s32[32,2048]{1,0:T(8,128)S(1)}, s32[32,2048]{1,0:T(8,128)}, u32[]{:S(2)}) copy-start(s32[32,2048]{1,0:T(8,128)} %param.15) | copy-start | bytes 786436
  9.5 23.3 %copy-start.5 = (bf16[32,2048]{1,0:T(8,128)(2,1)S(1)}, bf16[32,2048]{1,0:T(8,128)(2,1)}, u32[]{:S(2)}) copy-start(bf16[32,2048]{1,0:T(8,128)(2,1)} %param.9) | copy-start | bytes 393220
  11.6 44.5 %all-to-all-start = ((bf16[16,4,16,256]{3,2,1,0:T(8,128)(2,1)}), bf16[16,4,16,256]{3,2,1,0:T(8,128)(2,1)S(1)}, u32[]{:S(2)}, u32[]{:S(2)}) async-start(bf16[16,4,16,256]{3,2,1,0:T(8,128)(2,1)} %pad_maximum_fusion), calls=%async_computation | async-start | bytes 1048576 | tf_op jit(solution)/shard_map/all_to_all | solution.py:20
  20.8 89.7 %all-gather.9.cloned.1.call-start = ((), (), s32[]{:S(2)}) async-start(), calls=%async_computation.2 | async-start | bytes 2949120 | tf_op jit(solution)/shard_map/all_gather | solution.py:32
  56.8 1.2 copy-start.2
  56.8 1.5 copy-start.3
  63.2 101.7 %all-gather.11.cloned.1.call-start = ((), (), s32[]{:S(2)}) async-start(), calls=%async_computation.3 | async-start | bytes 2949120 | tf_op jit(solution)/shard_map/all_gather | solution.py:32
  111.8 2.9 %copy-start.1 = (f32[8,34,2048]{2,1,0:T(8,128)S(1)}, f32[8,34,2048]{2,1,0:T(8,128)}, u32[]{:S(2)}) copy-start(f32[8,34,2048]{2,1,0:T(8,128)} %all-gather.9.cloned.1.call-done) | copy-start | bytes 6684676
Sparse Core Ops, SparseCore 0:
  63.3 47.1 all-gather.8
  120.5 44.2 all-gather.10
where the time goes:
time: 190 us
  waiting for transfers between devices  91.6 us (48%)
  other arithmetic  44 us (23%)
  local copies, waits for them, and re-layouts  14.9 us (8%)
  between operations  14.3 us (8%)
  blocking collectives  11.6 us (6%)
  starting transfers between devices  9.42 us (5%)
  matrix products  3.82 us (2%)
    all_gather x2, waiting for transfers between devices, collected_together(): both, at, found = (lax.all_gather(jnp.concatenate(lines), axis), 0, {})  91.5 us
    reduce_sum x8, other arithmetic, on_device(): jnp.sum(jnp.where(match, token_fill[:, start:start + block, None], 0), ax...  22.4 us
    reduce_or x8, other arithmetic, on_device(): member = member | jnp.any(match, axis=1)  11.2 us
    all_to_all x1, blocking collectives, summed_on_arrival(): blocks = lax.all_to_all(split_up(shard, dim, count), axis, 0, 0, tiled=True)  9.37 us
    all_to_all x1, starting transfers between devices, side_by_side(): lax.all_to_all(both, axis, split_axis=split_dim, concat_axis=concat_dim,...  9.16 us
    unnamed x40, local copies, waits for them, and re-layouts  5.52 us
  transfers between devices with their start and end apart: 3, of which 2 were waited for; matrix products, arithmetic and copies ran while one was open for 19% of the time, Pallas kernels for 0%

commit v1 on v0

v1 whole, which is shorter than its diff:
```python
import functools
import math

import jax
import jax.numpy as jnp
from jax import lax
from jax.experimental import pallas as pl
from jax.experimental.pallas import tpu as pltpu
from jax.sharding import PartitionSpec as P

HD = 128
PAGE = 16
LANES = 128
CORES = 2
MESH = pl.DeviceIdType.MESH
VERY_LOW = -1.0e30
SCALE2 = HD**-0.5 * math.log2(math.e)
NT = (((1,), (1,)), ((), ()))


def lanes_of(shape):
    return lax.broadcasted_iota(jnp.int32, shape, len(shape) - 1)


def rows_of(shape):
    return lax.broadcasted_iota(jnp.int32, shape, len(shape) - 2)


def lane_sum(x):
    return jnp.sum(x.astype(jnp.float32), axis=1, keepdims=True).astype(jnp.int32)


def lane_or(words):
    low = lane_sum(words & 0xFFFF)
    high = lane_sum(lax.shift_right_logical(words, 16) & 0xFFFF)
    return low, high


def build_bias(tbl, pm, lens, tgt, bias, gi, z, n_page, slots, new_dev):
    seqs, pages = tbl.shape
    total = pm.shape[1]
    shard = gi * n_page + z
    base = shard * slots
    eye = rows_of((seqs, seqs)) == lanes_of((seqs, seqs))
    length = lane_sum(jnp.where(eye, lens[...], 0))
    used = (length + (PAGE - 1)) >> 4
    fill = length - (used - 1) * PAGE
    target = pm[0:1, :]
    slot = pm[1:2, :]
    number = lanes_of((1, total))
    sheet = (number // new_dev) % n_page
    valid = (target == gi) & (sheet == z)
    off = shard * new_dev
    own = jnp.where(
        lanes_of((new_dev, total)) == rows_of((new_dev, total)) + off,
        (target * n_page + z) * slots + slot,
        0,
    )
    tgt[...] = jnp.broadcast_to(lane_sum(own), tgt.shape)
    stale = []
    for w in range(slots // 16):
        hit = valid & ((slot >> 4) == w)
        stale.append(lane_sum(jnp.where(hit, jnp.int32(1) << (slot & 15), 0)))
    shape = (seqs, LANES)
    used_b = jnp.broadcast_to(used, shape)
    words = [jnp.zeros(shape, jnp.int32) for _ in range(slots // 32)]
    fresh = jnp.zeros(shape, jnp.int32)
    last = jnp.zeros(shape, jnp.int32)
    marks = [jnp.broadcast_to(tgt[k : k + 1, :], shape) for k in range(new_dev)]
    for c in range(pages // LANES):
        entry = tbl[:, c * LANES : (c + 1) * LANES]
        j = lanes_of(shape) + c * LANES
        last = last + jnp.where(j == used_b - 1, entry, 0)
        entry = jnp.where(j < used_b, entry, -1)
        local = entry - base
        high = local >> 5
        bit = jnp.int32(1) << (local & 31)
        for w in range(slots // 32):
            words[w] = words[w] | jnp.where(high == w, bit, 0)
        for k in range(new_dev):
            fresh = fresh | jnp.where(entry == marks[k], 1 << k, 0)
    last_b = jnp.broadcast_to(lane_sum(last), shape)
    fill_b = jnp.broadcast_to(fill, shape)
    owned = []
    for w in range(slots // 32):
        owned.extend(lane_or(words[w]))
    fresh_b = jnp.broadcast_to(lane_sum(fresh), shape)
    last_fresh = jnp.zeros(shape, jnp.int32)
    for k in range(new_dev):
        last_fresh = last_fresh | jnp.where(last_b == marks[k], 1 << k, 0)
    lane = lanes_of(shape)
    tail_end = (last_b - base) * PAGE + PAGE
    tail_start = tail_end - PAGE + fill_b
    per_tile = LANES // PAGE
    for w in range(slots // 16):
        word = jnp.broadcast_to(owned[w] & ~stale[w], shape)
        for half in range(16 // per_tile):
            c = w * (16 // per_tile) + half
            token = lane + c * LANES
            here = (lax.shift_right_logical(word, (lane >> 4) + half * per_tile) & 1) == 1
            here = here & ((token < tail_start) | (token >= tail_end))
            bias[:, c * LANES : (c + 1) * LANES] = jnp.where(here, 0.0, VERY_LOW)
    first = slots * PAGE
    for c in range(new_dev // per_tile):
        shift = (lane >> 4) + c * per_tile
        here = (lax.shift_right_logical(fresh_b, shift) & 1) == 1
        ends = (lax.shift_right_logical(last_fresh, shift) & 1) == 1
        here = here & ~(ends & ((lane & 15) >= fill_b))
        bias[:, first + c * LANES : first + (c + 1) * LANES] = jnp.where(here, 0.0, VERY_LOW)


def merge(stat_rows, values, rows):
    count = len(stat_rows)
    pad = [jnp.zeros((-count % 8, LANES), jnp.float32)] if count % 8 else []
    stats = jnp.concatenate(stat_rows + pad, axis=0)
    real = rows_of(stats.shape) < count
    highest = jnp.max(jnp.where(real, stats, -jnp.inf), axis=0, keepdims=True)
    in_max = lanes_of(stats.shape) < rows
    factor = jnp.where(real & in_max, jnp.exp2(jnp.where(in_max, stats - highest, 0.0)), 0.0)
    sums = pltpu.roll(stats, LANES - rows, 1)
    total = jnp.sum(factor * jnp.where(in_max, sums, 0.0), axis=0, keepdims=True)
    square = jnp.concatenate(
        [factor, jnp.broadcast_to(total, (8, LANES)), jnp.zeros((LANES - 8 - stats.shape[0], LANES), jnp.float32)],
        axis=0,
    )
    across = square.T
    mixed = across[:rows, 0:1] * values[0].astype(jnp.float32)
    for k in range(1, count):
        mixed = mixed + across[:rows, k : k + 1] * values[k].astype(jnp.float32)
    total_column = across[:rows, stats.shape[0] : stats.shape[0] + 1]
    return highest, total, total_column, mixed


def kernel(
    dims,
    q_in,
    ck_in,
    cv_in,
    nk_in,
    nv_in,
    pm_in,
    tbl_in,
    len_in,
    w_in,
    out_ref,
    q,
    key,
    value,
    pm,
    tbl,
    lens,
    weight,
    tgt,
    bias,
    scores,
    probs,
    tops,
    part_a,
    part_b,
    stat_a,
    stat_b,
    got_a,
    got_b,
    gots_a,
    gots_b,
    mid_a,
    mid_b,
    mids_a,
    mids_b,
    gotm_a,
    gotm_b,
    gotms_a,
    gotms_b,
    att_a,
    att_b,
    last_out,
    last_in,
    local_sem,
    send_sem,
    recv_sem,
):
    n_group, n_page, n_tensor, slots, new_dev = dims
    n_y = n_group // CORES
    gi = lax.axis_index("group")
    z = lax.axis_index("page")
    x = lax.axis_index("tensor")
    y = gi // CORES
    core = gi % CORES
    seqs = q.shape[0]
    kv_heads = key.shape[1] // HD
    share = q.shape[1] // HD // kv_heads
    rows = share * seqs
    cache_rows = slots * PAGE

    copies = []

    def fetch(src, dst):
        copy = pltpu.make_async_copy(src, dst, local_sem.at[len(copies)])
        copy.start()
        copies.append(copy)

    fetch(len_in, lens)
    fetch(pm_in, pm)
    fetch(tbl_in, tbl)
    fetch(q_in, q)
    fetch(ck_in, key.at[pl.ds(0, cache_rows)])
    fetch(nk_in, key.at[pl.ds(cache_rows, new_dev * PAGE)])
    fetch(cv_in, value.at[pl.ds(0, cache_rows)])
    fetch(nv_in, value.at[pl.ds(cache_rows, new_dev * PAGE)])
    fetch(w_in, weight)

    def along_group(d):
        return {"group": (gi + d) % n_group}

    def along_sheet(d):
        other = (z * CORES + core + d) % (n_page * CORES)
        return {"group": y * CORES + other % CORES, "page": other // CORES}

    def along_page(d):
        return {"page": (z + d) % n_page}

    def along_y(d):
        return {"group": (y + d) % n_y * CORES + core}

    def along_tensor(d):
        return {"tensor": (x + d) % n_tensor}

    n_sheet = n_page * CORES
    place_b = z * CORES + core
    greeted = [along_group(d) for d in range(1, n_group)]
    for d in range(1, n_sheet):
        if d % CORES == 0:
            greeted.append(along_sheet(d))
    greeted_cross = [d for d in range(1, n_sheet) if d % CORES]
    greeted += [along_tensor(d) for d in range(1, n_tensor)]
    barrier = pltpu.get_barrier_semaphore()
    for peer in greeted:
        pl.semaphore_signal(barrier, inc=1, device_id=peer, device_id_type=MESH)
    for d in greeted_cross:
        pl.semaphore_signal(barrier, inc=1, device_id=along_sheet(d), device_id_type=MESH)

    used = [0]

    def send(src, dst, peer):
        at = used[0]
        used[0] += 1
        copy = pltpu.make_async_remote_copy(
            src_ref=src,
            dst_ref=dst,
            send_sem=send_sem.at[at],
            recv_sem=recv_sem.at[at],
            device_id=peer,
            device_id_type=MESH,
        )
        copy.start()
        return copy

    for k in range(3):
        copies[k].wait()
    build_bias(tbl, pm, lens, tgt, bias, gi, z, n_page, slots, new_dev)
    for k in range(3, 6):
        copies[k].wait()
    for half in range(kv_heads):
        heads = range(half * share, (half + 1) * share)
        stacked = jnp.concatenate([q[:, h * HD : (h + 1) * HD] for h in heads], axis=0)
        scores[half] = lax.dot_general(
            stacked,
            key[:, half * HD : (half + 1) * HD],
            NT,
            preferred_element_type=jnp.float32,
        )
    for k in range(6, 8):
        copies[k].wait()

    def far_first(count):
        return sorted(range(1, count), key=lambda d: -min(d, count - d))

    def attend(half, part, stat):
        count, own_rows = part.shape[0], part.shape[1]
        block = 16
        for b in range(rows // block):
            s0 = b * block % seqs
            s = scores[half, b * block : (b + 1) * block, :] * SCALE2 + bias[s0 : s0 + block, :]
            top = jnp.max(s, axis=1, keepdims=True)
            probs[b * block : (b + 1) * block, :] = jnp.exp2(s - top).astype(jnp.bfloat16)
            tops[b * block : (b + 1) * block, :] = jnp.broadcast_to(top, (block, LANES))
        v = value[:, half * HD : (half + 1) * HD]
        wide = jnp.concatenate([v, jnp.ones_like(v)], axis=1)
        summed = jnp.dot(probs[...], wide, preferred_element_type=jnp.float32)
        shape = (own_rows, LANES)
        lane, row = lanes_of(shape), rows_of(shape)
        for k in range(count):
            at = slice(k * own_rows, (k + 1) * own_rows)
            part[k] = summed[at, :HD].astype(jnp.bfloat16)
            picked = jnp.where(lane == row, tops[at, :], jnp.where(lane == row + own_rows, summed[at, HD:], 0.0))
            stat[k] = jnp.sum(picked, axis=0, keepdims=True)

    def scatter(part, stat, got, gots, place, peer_of):
        count = part.shape[0]
        sent = {}
        for d in far_first(count):
            owner = (place + d) % count
            sent[d] = (
                send(part.at[owner], got.at[d - 1], peer_of(d)),
                send(stat.at[owner], gots.at[d - 1], peer_of(d)),
            )
        return sent

    def merge_scattered(sent, part, stat, got, gots, mid, mids, place):
        own_rows = part.shape[1]
        for d in sent:
            for copy in sent[d]:
                copy.wait_recv()
        stats = [stat[place]] + [gots[d - 1] for d in sorted(sent)]
        values = [part[place]] + [got[d - 1] for d in sorted(sent)]
        highest, total, _, mixed = merge(stats, values, own_rows)
        mid[...] = mixed.astype(jnp.bfloat16)
        low = lanes_of((1, LANES)) < own_rows
        mids[...] = jnp.where(low, highest, pltpu.roll(total, own_rows, 1))

    def spread(mid, mids, gotm, gotms, peer_of):
        sent = {}
        for d in far_first(gotm.shape[0] + 1):
            sent[d] = (send(mid, gotm.at[d - 1], peer_of(d)), send(mids, gotms.at[d - 1], peer_of(d)))
        return sent

    def merge_spread(sent, mid, mids, gotm, gotms, att, place):
        for d in sent:
            for copy in sent[d]:
                copy.wait_recv()
        stats = [mids[...]] + [gotms[d - 1] for d in sorted(sent)]
        values = [mid[...]] + [gotm[d - 1] for d in sorted(sent)]
        _, _, total_column, mixed = merge(stats, values, mid.shape[0])
        att[place] = (mixed / total_column).astype(jnp.bfloat16)

    def gather(att, place, peer_of):
        return {d: (send(att.at[place], att.at[place], peer_of(d)),) for d in far_first(att.shape[0])}

    def finish(sent):
        for d in sent:
            for copy in sent[d]:
                copy.wait_send()

    attend(0, part_a, stat_a)
    pl.semaphore_wait(barrier, len(greeted) + len(greeted_cross))
    first_a = scatter(part_a, stat_a, got_a, gots_a, gi, along_group)
    attend(1, part_b, stat_b)
    first_b = scatter(part_b, stat_b, got_b, gots_b, place_b, along_sheet)
    merge_scattered(first_a, part_a, stat_a, got_a, gots_a, mid_a, mids_a, gi)
    second_a = spread(mid_a, mids_a, gotm_a, gotms_a, along_page)
    merge_scattered(first_b, part_b, stat_b, got_b, gots_b, mid_b, mids_b, place_b)
    second_b = spread(mid_b, mids_b, gotm_b, gotms_b, along_y)
    finish(first_a)
    finish(first_b)
    merge_spread(second_a, mid_a, mids_a, gotm_a, gotms_a, att_a, gi)
    third_a = gather(att_a, gi, along_group)
    merge_spread(second_b, mid_b, mids_b, gotm_b, gotms_b, att_b, place_b)
    third_b = gather(att_b, place_b, along_sheet)
    finish(second_a)
    finish(second_b)
    copies[8].wait()
    for sent in (third_a, third_b):
        for d in sent:
            for copy in sent[d]:
                copy.wait_recv()
    pieces = []
    for att in (att_a, att_b):
        flat = att[...].reshape(rows, HD)
        pieces += [flat[h * seqs : (h + 1) * seqs] for h in range(share)]
    features = jnp.concatenate(pieces, axis=1)
    last_out[...] = lax.dot_general(features, weight[...], NT, preferred_element_type=jnp.float32)
    fourth = {d: (send(last_out, last_in.at[d - 1], along_tensor(d)),) for d in far_first(n_tensor)}
    finish(third_a)
    finish(third_b)
    for d in fourth:
        for copy in fourth[d]:
            copy.wait_recv()
    result = last_out[...]
    for d in range(1, n_tensor):
        result = result + last_in[d - 1]
    width = out_ref.shape[1]
    mine = result[:, :width]
    for t in range(1, n_tensor):
        mine = jnp.where(x == t, result[:, t * width : (t + 1) * width], mine)
    out_ref[...] = mine.astype(out_ref.dtype)
    finish(fourth)


def on_device(sizes, query, cache_keys, cache_values, new_keys, new_values, page_map, page_table, lengths, out_weight):
    n_group, n_page, n_tensor = sizes
    slots, page, width = cache_keys.shape
    new_dev = new_keys.shape[0]
    seqs = query.shape[0]
    tokens = (slots + new_dev) * page
    kv_heads = width // HD
    share = query.shape[1] // HD // kv_heads
    rows = share * seqs
    n_sheet = n_page * CORES
    n_y = n_group // CORES
    columns = out_weight.shape[1]
    rows_a, rows_b = rows // n_group, rows // n_sheet
    bf16, f32 = jnp.bfloat16, jnp.float32
    copies = 2 * (n_group - 1) + 2 * (n_sheet - 1) + 2 * (n_page - 1) + 2 * (n_y - 1)
    copies += (n_group - 1) + (n_sheet - 1) + (n_tensor - 1)
    scratch = [
        pltpu.VMEM(query.shape, bf16),
        pltpu.VMEM((tokens, width), bf16),
        pltpu.VMEM((tokens, width), bf16),
        pltpu.VMEM((2, page_map.shape[0]), jnp.int32),
        pltpu.VMEM(page_table.shape, jnp.int32),
        pltpu.VMEM((1, seqs), jnp.int32),
        pltpu.VMEM((columns, out_weight.shape[0]), bf16),
        pltpu.VMEM((new_dev, LANES), jnp.int32),
        pltpu.VMEM((seqs, tokens), f32),
        pltpu.VMEM((kv_heads, rows, tokens), f32),
        pltpu.VMEM((rows, tokens), bf16),
        pltpu.VMEM((rows, LANES), f32),
        pltpu.VMEM((n_group, rows_a, HD), bf16),
        pltpu.VMEM((n_sheet, rows_b, HD), bf16),
        pltpu.VMEM((n_group, 1, LANES), f32),
        pltpu.VMEM((n_sheet, 1, LANES), f32),
        pltpu.VMEM((n_group - 1, rows_a, HD), bf16),
        pltpu.VMEM((n_sheet - 1, rows_b, HD), bf16),
        pltpu.VMEM((n_group - 1, 1, LANES), f32),
        pltpu.VMEM((n_sheet - 1, 1, LANES), f32),
        pltpu.VMEM((rows_a, HD), bf16),
        pltpu.VMEM((rows_b, HD), bf16),
        pltpu.VMEM((1, LANES), f32),
        pltpu.VMEM((1, LANES), f32),
        pltpu.VMEM((n_page - 1, rows_a, HD), bf16),
        pltpu.VMEM((n_y - 1, rows_b, HD), bf16),
        pltpu.VMEM((n_page - 1, 1, LANES), f32),
        pltpu.VMEM((n_y - 1, 1, LANES), f32),
        pltpu.VMEM((n_group, rows_a, HD), bf16),
        pltpu.VMEM((n_sheet, rows_b, HD), bf16),
        pltpu.VMEM((seqs, columns), f32),
        pltpu.VMEM((n_tensor - 1, seqs, columns), f32),
        pltpu.SemaphoreType.DMA((9,)),
        pltpu.SemaphoreType.DMA((copies,)),
        pltpu.SemaphoreType.DMA((copies,)),
    ]
    return pl.pallas_call(
        functools.partial(kernel, (n_group, n_page, n_tensor, slots, new_dev)),
        out_shape=jax.ShapeDtypeStruct((seqs, columns // n_tensor), bf16),
        in_specs=[pl.BlockSpec(memory_space=pl.ANY)] * 9,
        out_specs=pl.BlockSpec(memory_space=pltpu.VMEM),
        scratch_shapes=scratch,
        compiler_params=pltpu.CompilerParams(
            collective_id=0, has_side_effects=True, vmem_limit_bytes=40 * 1024 * 1024
        ),
    )(
        query,
        cache_keys.reshape(slots * page, width),
        cache_values.reshape(slots * page, width),
        new_keys.reshape(new_dev * page, width),
        new_values.reshape(new_dev * page, width),
        page_map.T,
        page_table,
        lengths.reshape(1, seqs),
        out_weight.T,
    )


def solution(mesh):
    shards = ("group", "page")
    sizes = (mesh.shape["group"], mesh.shape["page"], mesh.shape["tensor"])
    placed = (
        P(None, "tensor"),
        P(shards, None, "tensor"),
        P(shards, None, "tensor"),
        P(shards, None, "tensor"),
        P(shards, None, "tensor"),
        P(),
        P(),
        P(),
        P("tensor", shards),
    )
    return jax.shard_map(
        functools.partial(on_device, sizes),
        mesh=mesh,
        in_specs=placed,
        out_specs=P(None, ("group", "page", "tensor")),
        check_vma=False,
    )
```

time: 190 us -> 47.4 us (0.25)
  the two profiles are of different devices: /device:TPU:8 before, /device:TPU:1 now
where the time goes in v1:
time: 47.4 us; the launch traced here: 47 us
  Pallas kernels  37.9 us (80%)
  local copies, waits for them, and re-layouts  9.1 us (19%)
    pallas_call x1, Pallas kernels, on_device(): pl.pallas_call(functools.partial(kernel, (n_group, n_page, n_tensor, slot...  37.9 us
    unnamed x18, local copies, waits for them, and re-layouts  8.43 us

profile of v1, /device:TPU:1, one launch (start us, length us, event | category | flops | bytes accessed | tf_op | source)
XLA Modules:
  0.0 47.0 jit_solution(4143101687385844259)
XLA Ops:
  0.0 0.0 copy-start.8
  0.0 0.7 %copy-done.8 = s32[32]{0:T(128)S(1)} copy-done((s32[32]{0:T(128)S(1)}, s32[32]{0:T(128)}, u32[]{:S(2)}) %copy-start.8) | copy-done | bytes 152
  0.7 0.0 copy-start
  0.7 1.2 %copy-done = bf16[128,16,256]{2,1,0:T(8,128)(2,1)S(1)} copy-done((bf16[128,16,256]{2,1,0:T(8,128)(2,1)S(1)}, bf16[128,16,256]{2,1,0:T(8,128)(2,1)}, u32[]{:S(2)}) %copy-start) | copy-done | bytes 1048600
  1.9 0.0 copy-start.1
  1.9 1.2 %copy-done.1 = bf16[128,16,256]{2,1,0:T(8,128)(2,1)S(1)} copy-done((bf16[128,16,256]{2,1,0:T(8,128)(2,1)S(1)}, bf16[128,16,256]{2,1,0:T(8,128)(2,1)}, u32[]{:S(2)}) %copy-start.1) | copy-done | bytes 1048600
  3.1 0.0 copy-start.2
  3.1 0.9 %copy-done.2 = s32[32,2048]{1,0:T(8,128)S(1)} copy-done((s32[32,2048]{1,0:T(8,128)S(1)}, s32[32,2048]{1,0:T(8,128)}, u32[]{:S(2)}) %copy-start.2) | copy-done | bytes 262168
  4.1 0.0 copy-start.3
  4.1 0.9 %copy-done.3 = bf16[2048,64]{0,1:T(8,128)(2,1)S(1)} copy-done((bf16[2048,64]{0,1:T(8,128)(2,1)S(1)}, bf16[2048,64]{0,1:T(8,128)(2,1)}, u32[]{:S(2)}) %copy-start.3) | copy-done | bytes 262168
  5.0 0.0 copy-start.4
  5.0 0.9 %copy-done.4 = bf16[32,2048]{1,0:T(8,128)(2,1)S(1)} copy-done((bf16[32,2048]{1,0:T(8,128)(2,1)S(1)}, bf16[32,2048]{1,0:T(8,128)(2,1)}, u32[]{:S(2)}) %copy-start.4) | copy-done | bytes 131096
  5.9 0.0 copy-start.5
  5.9 0.9 %copy-done.5 = bf16[16,16,256]{2,1,0:T(8,128)(2,1)S(1)} copy-done((bf16[16,16,256]{2,1,0:T(8,128)(2,1)S(1)}, bf16[16,16,256]{2,1,0:T(8,128)(2,1)}, u32[]{:S(2)}) %copy-start.5) | copy-done | bytes 131096
  6.8 0.0 copy-start.6
  6.8 0.9 %copy-done.6 = bf16[16,16,256]{2,1,0:T(8,128)(2,1)S(1)} copy-done((bf16[16,16,256]{2,1,0:T(8,128)(2,1)S(1)}, bf16[16,16,256]{2,1,0:T(8,128)(2,1)}, u32[]{:S(2)}) %copy-start.6) | copy-done | bytes 131096
  7.7 0.0 copy-start.7
  7.7 0.7 %copy-done.7 = s32[2048,2]{0,1:T(2,128)S(1)} copy-done((s32[2048,2]{0,1:T(2,128)S(1)}, s32[2048,2]{0,1:T(2,128)}, u32[]{:S(2)}) %copy-start.7) | copy-done | bytes 16408
  8.4 37.9 %shard_map.91 = bf16[32,16]{1,0:T(8,128)(2,1)S(1)} custom-call(bf16[32,2048]{1,0:T(8,128)(2,1)S(1)} %copy-done.4, bf16[2048,256]{1,0:T(8,128)(2,1)S(1)} %bitcast.7, bf16[2048,256]{1,0:T(8,128)(2,1)S(1)} %bitcast.8, bf16[256,256]{1,0:T(8,128)(2,1)S(1)} %bitcast.10, bf16[256,256]{1,0:T(8,128)(2,1)S(1)} %bitcast.11, s32[2,2048]{1,0:T(2,128)S(1)} %bitcast.12, ...), custom_call_target="tpu_custom_call" | custom-call | tf_op jit(solution)/shard_map/pallas_call | solution.py:442
  46.4 0.7 %copy.10 = bf16[32,16]{0,1:T(8,128)(2,1)} copy(bf16[32,16]{1,0:T(8,128)(2,1)S(1)} %shard_map.91) | data formatting | bytes 2048 | tf_op jit(solution)/shard_map/pallas_call | solution.py:442
Async XLA Ops:
  0.0 0.7 %copy-start.8 = (s32[32]{0:T(128)S(1)}, s32[32]{0:T(128)}, u32[]{:S(2)}) copy-start(s32[32]{0:T(128)} %param.16) | copy-start | bytes 388
  0.7 1.2 %copy-start = (bf16[128,16,256]{2,1,0:T(8,128)(2,1)S(1)}, bf16[128,16,256]{2,1,0:T(8,128)(2,1)}, u32[]{:S(2)}) copy-start(bf16[128,16,256]{2,1,0:T(8,128)(2,1)} %param.10) | copy-start | bytes 3145732
  1.9 1.2 %copy-start.1 = (bf16[128,16,256]{2,1,0:T(8,128)(2,1)S(1)}, bf16[128,16,256]{2,1,0:T(8,128)(2,1)}, u32[]{:S(2)}) copy-start(bf16[128,16,256]{2,1,0:T(8,128)(2,1)} %param.11) | copy-start | bytes 3145732
  3.1 0.9 %copy-start.2 = (s32[32,2048]{1,0:T(8,128)S(1)}, s32[32,2048]{1,0:T(8,128)}, u32[]{:S(2)}) copy-start(s32[32,2048]{1,0:T(8,128)} %tbl_in.1) | copy-start | bytes 786436
  4.1 0.9 %copy-start.3 = (bf16[2048,64]{0,1:T(8,128)(2,1)S(1)}, bf16[2048,64]{0,1:T(8,128)(2,1)}, u32[]{:S(2)}) copy-start(bf16[2048,64]{0,1:T(8,128)(2,1)} %param.17) | copy-start | bytes 786436
  5.0 0.9 %copy-start.4 = (bf16[32,2048]{1,0:T(8,128)(2,1)S(1)}, bf16[32,2048]{1,0:T(8,128)(2,1)}, u32[]{:S(2)}) copy-start(bf16[32,2048]{1,0:T(8,128)(2,1)} %q_in.1) | copy-start | bytes 393220
  5.9 0.9 %copy-start.5 = (bf16[16,16,256]{2,1,0:T(8,128)(2,1)S(1)}, bf16[16,16,256]{2,1,0:T(8,128)(2,1)}, u32[]{:S(2)}) copy-start(bf16[16,16,256]{2,1,0:T(8,128)(2,1)} %param.12) | copy-start | bytes 393220
  6.8 0.9 %copy-start.6 = (bf16[16,16,256]{2,1,0:T(8,128)(2,1)S(1)}, bf16[16,16,256]{2,1,0:T(8,128)(2,1)}, u32[]{:S(2)}) copy-start(bf16[16,16,256]{2,1,0:T(8,128)(2,1)} %param.13) | copy-start | bytes 393220
  7.7 0.7 %copy-start.7 = (s32[2048,2]{0,1:T(2,128)S(1)}, s32[2048,2]{0,1:T(2,128)}, u32[]{:S(2)}) copy-start(s32[2048,2]{0,1:T(2,128)} %param.14) | copy-start | bytes 49156

commit v2 on v1

--- a/solution.py
+++ b/solution.py
@@ -64,9 +64,11 @@
     shape = (seqs, LANES)
     used_b = jnp.broadcast_to(used, shape)
     words = [jnp.zeros(shape, jnp.int32) for _ in range(slots // 32)]
-    fresh = jnp.zeros(shape, jnp.int32)
+    fresh = jnp.zeros(shape, jnp.int16)
     last = jnp.zeros(shape, jnp.int32)
     marks = [jnp.broadcast_to(tgt[k : k + 1, :], shape) for k in range(new_dev)]
+    narrow_marks = [m.astype(jnp.int16) for m in marks]
+    narrow_bits = [jnp.int16((1 << k) if k < 15 else -(1 << 15)) for k in range(new_dev)]
     for c in range(pages // LANES):
         entry = tbl[:, c * LANES : (c + 1) * LANES]
         j = lanes_of(shape) + c * LANES
@@ -77,14 +79,15 @@
         bit = jnp.int32(1) << (local & 31)
         for w in range(slots // 32):
             words[w] = words[w] | jnp.where(high == w, bit, 0)
+        narrow = entry.astype(jnp.int16)
         for k in range(new_dev):
-            fresh = fresh | jnp.where(entry == marks[k], 1 << k, 0)
+            fresh = fresh | jnp.where(narrow == narrow_marks[k], narrow_bits[k], jnp.int16(0))
     last_b = jnp.broadcast_to(lane_sum(last), shape)
     fill_b = jnp.broadcast_to(fill, shape)
     owned = []
     for w in range(slots // 32):
         owned.extend(lane_or(words[w]))
-    fresh_b = jnp.broadcast_to(lane_sum(fresh), shape)
+    fresh_b = jnp.broadcast_to(lane_sum(fresh.astype(jnp.int32) & 0xFFFF), shape)
     last_fresh = jnp.zeros(shape, jnp.int32)
     for k in range(new_dev):
         last_fresh = last_fresh | jnp.where(last_b == marks[k], 1 << k, 0)
@@ -184,8 +187,8 @@
     gi = lax.axis_index("group")
     z = lax.axis_index("page")
     x = lax.axis_index("tensor")
-    y = gi // CORES
-    core = gi % CORES
+    y = lax.div(gi, CORES)
+    core = lax.rem(gi, CORES)
     seqs = q.shape[0]
     kv_heads = key.shape[1] // HD
     share = q.shape[1] // HD // kv_heads
@@ -210,20 +213,20 @@
     fetch(w_in, weight)
 
     def along_group(d):
-        return {"group": (gi + d) % n_group}
+        return {"group": lax.rem(gi + d, n_group)}
 
     def along_sheet(d):
-        other = (z * CORES + core + d) % (n_page * CORES)
-        return {"group": y * CORES + other % CORES, "page": other // CORES}
+        other = lax.rem(z * CORES + core + d, n_page * CORES)
+        return {"group": y * CORES + lax.rem(other, CORES), "page": lax.div(other, CORES)}
 
     def along_page(d):
-        return {"page": (z + d) % n_page}
+        return {"page": lax.rem(z + d, n_page)}
 
     def along_y(d):
-        return {"group": (y + d) % n_y * CORES + core}
+        return {"group": lax.rem(y + d, n_y) * CORES + core}
 
     def along_tensor(d):
-        return {"tensor": (x + d) % n_tensor}
+        return {"tensor": lax.rem(x + d, n_tensor)}
 
     n_sheet = n_page * CORES
     place_b = z * CORES + core
@@ -239,26 +242,23 @@
     for d in greeted_cross:
         pl.semaphore_signal(barrier, inc=1, device_id=along_sheet(d), device_id_type=MESH)
 
-    used = [0]
-
-    def send(src, dst, peer):
-        at = used[0]
-        used[0] += 1
-        copy = pltpu.make_async_remote_copy(
+    def send(src, dst, peer, at):
+        pltpu.make_async_remote_copy(
             src_ref=src,
             dst_ref=dst,
             send_sem=send_sem.at[at],
             recv_sem=recv_sem.at[at],
             device_id=peer,
             device_id_type=MESH,
-        )
-        copy.start()
-        return copy
-
-    for k in range(3):
-        copies[k].wait()
-    build_bias(tbl, pm, lens, tgt, bias, gi, z, n_page, slots, new_dev)
-    for k in range(3, 6):
+        ).start()
+
+    def received(ref, at):
+        pltpu.make_async_copy(ref, ref, recv_sem.at[at]).wait()
+
+    def left(ref, at):
+        pltpu.make_async_copy(ref, ref, send_sem.at[at]).wait()
+
+    for k in range(6):
         copies[k].wait()
     for half in range(kv_heads):
         heads = range(half * share, (half + 1) * share)
@@ -269,121 +269,122 @@
             NT,
             preferred_element_type=jnp.float32,
         )
+    build_bias(tbl, pm, lens, tgt, bias, gi, z, n_page, slots, new_dev)
     for k in range(6, 8):
         copies[k].wait()
 
     def far_first(count):
         return sorted(range(1, count), key=lambda d: -min(d, count - d))
 
-    def attend(half, part, stat):
-        count, own_rows = part.shape[0], part.shape[1]
+    def soften(half):
         block = 16
         for b in range(rows // block):
             s0 = b * block % seqs
-            s = scores[half, b * block : (b + 1) * block, :] * SCALE2 + bias[s0 : s0 + block, :]
+            at = slice(b * block, (b + 1) * block)
+            s = scores[half, at, :] * SCALE2 + bias[s0 : s0 + block, :]
             top = jnp.max(s, axis=1, keepdims=True)
-            probs[b * block : (b + 1) * block, :] = jnp.exp2(s - top).astype(jnp.bfloat16)
-            tops[b * block : (b + 1) * block, :] = jnp.broadcast_to(top, (block, LANES))
+            probs[half, at, :] = jnp.exp2(s - top).astype(jnp.bfloat16)
+            tops[half, at, :] = jnp.broadcast_to(top, (block, LANES))
+
+    def weigh(half, part, stat):
+        count, own_rows = part.shape[0], part.shape[1]
         v = value[:, half * HD : (half + 1) * HD]
         wide = jnp.concatenate([v, jnp.ones_like(v)], axis=1)
-        summed = jnp.dot(probs[...], wide, preferred_element_type=jnp.float32)
+        summed = jnp.dot(probs[half], wide, preferred_element_type=jnp.float32)
         shape = (own_rows, LANES)
         lane, row = lanes_of(shape), rows_of(shape)
         for k in range(count):
             at = slice(k * own_rows, (k + 1) * own_rows)
             part[k] = summed[at, :HD].astype(jnp.bfloat16)
-            picked = jnp.where(lane == row, tops[at, :], jnp.where(lane == row + own_rows, summed[at, HD:], 0.0))
+            sums = jnp.where(lane == row + own_rows, summed[at, HD:], 0.0)
+            picked = jnp.where(lane == row, tops[half, at, :], sums)
             stat[k] = jnp.sum(picked, axis=0, keepdims=True)
 
-    def scatter(part, stat, got, gots, place, peer_of):
+    def scatter(part, stat, got, gots, place, peer_of, at):
         count = part.shape[0]
-        sent = {}
         for d in far_first(count):
-            owner = (place + d) % count
-            sent[d] = (
-                send(part.at[owner], got.at[d - 1], peer_of(d)),
-                send(stat.at[owner], gots.at[d - 1], peer_of(d)),
-            )
-        return sent
-
-    def merge_scattered(sent, part, stat, got, gots, mid, mids, place):
-        own_rows = part.shape[1]
-        for d in sent:
-            for copy in sent[d]:
-                copy.wait_recv()
-        stats = [stat[place]] + [gots[d - 1] for d in sorted(sent)]
-        values = [part[place]] + [got[d - 1] for d in sorted(sent)]
+            owner = lax.rem(place + d, count)
+            send(part.at[owner], got.at[d - 1], peer_of(d), at)
+            send(stat.at[owner], gots.at[d - 1], peer_of(d), at + 1)
+
+    def merge_scattered(part, stat, got, gots, mid, mids, place, at):
+        count, own_rows = part.shape[0], part.shape[1]
+        received(got, at)
+        received(gots, at + 1)
+        stats = [stat[place]] + [gots[d - 1] for d in range(1, count)]
+        values = [part[place]] + [got[d - 1] for d in range(1, count)]
         highest, total, _, mixed = merge(stats, values, own_rows)
         mid[...] = mixed.astype(jnp.bfloat16)
         low = lanes_of((1, LANES)) < own_rows
         mids[...] = jnp.where(low, highest, pltpu.roll(total, own_rows, 1))
 
-    def spread(mid, mids, gotm, gotms, peer_of):
-        sent = {}
+    def spread(mid, mids, gotm, gotms, peer_of, at):
         for d in far_first(gotm.shape[0] + 1):
-            sent[d] = (send(mid, gotm.at[d - 1], peer_of(d)), send(mids, gotms.at[d - 1], peer_of(d)))
-        return sent
-
-    def merge_spread(sent, mid, mids, gotm, gotms, att, place):
-        for d in sent:
-            for copy in sent[d]:
-                copy.wait_recv()
-        stats = [mids[...]] + [gotms[d - 1] for d in sorted(sent)]
-        values = [mid[...]] + [gotm[d - 1] for d in sorted(sent)]
+            send(mid, gotm.at[d - 1], peer_of(d), at)
+            send(mids, gotms.at[d - 1], peer_of(d), at + 1)
+
+    def merge_spread(mid, mids, gotm, gotms, att, place, at):
+        received(gotm, at)
+        received(gotms, at + 1)
+        others = range(gotm.shape[0])
+        stats = [mids[...]] + [gotms[k] for k in others]
+        values = [mid[...]] + [gotm[k] for k in others]
         _, _, total_column, mixed = merge(stats, values, mid.shape[0])
         att[place] = (mixed / total_column).astype(jnp.bfloat16)
 
-    def gather(att, place, peer_of):
-        return {d: (send(att.at[place], att.at[place], peer_of(d)),) for d in far_first(att.shape[0])}
-
-    def finish(sent):
-        for d in sent:
-            for copy in sent[d]:
-                copy.wait_send()
-
-    attend(0, part_a, stat_a)
+    def gather(att, place, peer_of, at):
+        for d in far_first(att.shape[0]):
+            send(att.at[place], att.at[place], peer_of(d), at)
+
+    soften(0)
+    soften(1)
+    weigh(0, part_a, stat_a)
     pl.semaphore_wait(barrier, len(greeted) + len(greeted_cross))
-    first_a = scatter(part_a, stat_a, got_a, gots_a, gi, along_group)
-    attend(1, part_b, stat_b)
-    first_b = scatter(part_b, stat_b, got_b, gots_b, place_b, along_sheet)
-    merge_scattered(first_a, part_a, stat_a, got_a, gots_a, mid_a, mids_a, gi)
-    second_a = spread(mid_a, mids_a, gotm_a, gotms_a, along_page)
-    merge_scattered(first_b, part_b, stat_b, got_b, gots_b, mid_b, mids_b, place_b)
-    second_b = spread(mid_b, mids_b, gotm_b, gotms_b, along_y)
-    finish(first_a)
-    finish(first_b)
-    merge_spread(second_a, mid_a, mids_a, gotm_a, gotms_a, att_a, gi)
-    third_a = gather(att_a, gi, along_group)
-    merge_spread(second_b, mid_b, mids_b, gotm_b, gotms_b, att_b, place_b)
-    third_b = gather(att_b, place_b, along_sheet)
-    finish(second_a)
-    finish(second_b)
+    scatter(part_a, stat_a, got_a, gots_a, gi, along_group, 0)
+    weigh(1, part_b, stat_b)
+    scatter(part_b, stat_b, got_b, gots_b, place_b, along_sheet, 2)
+    merge_scattered(part_a, stat_a, got_a, gots_a, mid_a, mids_a, gi, 0)
+    spread(mid_a, mids_a, gotm_a, gotms_a, along_page, 4)
+    merge_scattered(part_b, stat_b, got_b, gots_b, mid_b, mids_b, place_b, 2)
+    spread(mid_b, mids_b, gotm_b, gotms_b, along_y, 6)
+    left(got_a, 0)
+    left(gots_a, 1)
+    left(got_b, 2)
+    left(gots_b, 3)
+    merge_spread(mid_a, mids_a, gotm_a, gotms_a, att_a, gi, 4)
+    gather(att_a, gi, along_group, 8)
+    merge_spread(mid_b, mids_b, gotm_b, gotms_b, att_b, place_b, 6)
+    gather(att_b, place_b, along_sheet, 9)
+    left(gotm_a, 4)
+    left(gotms_a, 5)
+    left(gotm_b, 6)
+    left(gotms_b, 7)
+    others_a = att_a.at[pl.ds(0, n_group - 1)]
+    others_b = att_b.at[pl.ds(0, n_sheet - 1)]
     copies[8].wait()
-    for sent in (third_a, third_b):
-        for d in sent:
-            for copy in sent[d]:
-                copy.wait_recv()
+    received(others_a, 8)
+    received(others_b, 9)
     pieces = []
     for att in (att_a, att_b):
         flat = att[...].reshape(rows, HD)
         pieces += [flat[h * seqs : (h + 1) * seqs] for h in range(share)]
     features = jnp.concatenate(pieces, axis=1)
-    last_out[...] = lax.dot_general(features, weight[...], NT, preferred_element_type=jnp.float32)
-    fourth = {d: (send(last_out, last_in.at[d - 1], along_tensor(d)),) for d in far_first(n_tensor)}
-    finish(third_a)
-    finish(third_b)
-    for d in fourth:
-        for copy in fourth[d]:
-            copy.wait_recv()
-    result = last_out[...]
+    last_out[...] = lax.dot_general(weight[...], features, NT, preferred_element_type=jnp.float32)
+    width = out_ref.shape[0]
+
+    def block_of(d):
+        return last_out.at[pl.ds(pl.multiple_of(lax.rem(x + d, n_tensor) * width, width), width)]
+
+    for d in far_first(n_tensor):
+        send(block_of(d), last_in.at[d - 1], along_tensor(d), 10)
+    left(others_a, 8)
+    left(others_b, 9)
+    received(last_in, 10)
+    result = block_of(0)[...]
     for d in range(1, n_tensor):
         result = result + last_in[d - 1]
-    width = out_ref.shape[1]
-    mine = result[:, :width]
-    for t in range(1, n_tensor):
-        mine = jnp.where(x == t, result[:, t * width : (t + 1) * width], mine)
-    out_ref[...] = mine.astype(out_ref.dtype)
-    finish(fourth)
+    out_ref[...] = result.astype(out_ref.dtype)
+    left(last_in, 10)
 
 
 def on_device(sizes, query, cache_keys, cache_values, new_keys, new_values, page_map, page_table, lengths, out_weight):
@@ -400,8 +401,6 @@
     columns = out_weight.shape[1]
     rows_a, rows_b = rows // n_group, rows // n_sheet
     bf16, f32 = jnp.bfloat16, jnp.float32
-    copies = 2 * (n_group - 1) + 2 * (n_sheet - 1) + 2 * (n_page - 1) + 2 * (n_y - 1)
-    copies += (n_group - 1) + (n_sheet - 1) + (n_tensor - 1)
     scratch = [
         pltpu.VMEM(query.shape, bf16),
         pltpu.VMEM((tokens, width), bf16),
@@ -413,8 +412,8 @@
         pltpu.VMEM((new_dev, LANES), jnp.int32),
         pltpu.VMEM((seqs, tokens), f32),
         pltpu.VMEM((kv_heads, rows, tokens), f32),
-        pltpu.VMEM((rows, tokens), bf16),
-        pltpu.VMEM((rows, LANES), f32),
+        pltpu.VMEM((kv_heads, rows, tokens), bf16),
+        pltpu.VMEM((kv_heads, rows, LANES), f32),
         pltpu.VMEM((n_group, rows_a, HD), bf16),
         pltpu.VMEM((n_sheet, rows_b, HD), bf16),
         pltpu.VMEM((n_group, 1, LANES), f32),
@@ -433,22 +432,22 @@
         pltpu.VMEM((n_y - 1, 1, LANES), f32),
         pltpu.VMEM((n_group, rows_a, HD), bf16),
         pltpu.VMEM((n_sheet, rows_b, HD), bf16),
-        pltpu.VMEM((seqs, columns), f32),
-        pltpu.VMEM((n_tensor - 1, seqs, columns), f32),
+        pltpu.VMEM((columns, seqs), f32),
+        pltpu.VMEM((n_tensor - 1, columns // n_tensor, seqs), f32),
         pltpu.SemaphoreType.DMA((9,)),
-        pltpu.SemaphoreType.DMA((copies,)),
-        pltpu.SemaphoreType.DMA((copies,)),
+        pltpu.SemaphoreType.DMA((11,)),
+        pltpu.SemaphoreType.DMA((11,)),
     ]
     return pl.pallas_call(
         functools.partial(kernel, (n_group, n_page, n_tensor, slots, new_dev)),
-        out_shape=jax.ShapeDtypeStruct((seqs, columns // n_tensor), bf16),
-        in_specs=[pl.BlockSpec(memory_space=pl.ANY)] * 9,
+        out_shape=pltpu.VMEM((columns // n_tensor, seqs), bf16),
+        in_specs=[pl.BlockSpec(memory_space=pltpu.HBM)] * 9,
         out_specs=pl.BlockSpec(memory_space=pltpu.VMEM),
         scratch_shapes=scratch,
         compiler_params=pltpu.CompilerParams(
             collective_id=0, has_side_effects=True, vmem_limit_bytes=40 * 1024 * 1024
         ),
-    )(
+    )(*[pltpu.with_memory_space_constraint(a, pltpu.HBM) for a in (
         query,
         cache_keys.reshape(slots * page, width),
         cache_values.reshape(slots * page, width),
@@ -458,7 +457,7 @@
         page_table,
         lengths.reshape(1, seqs),
         out_weight.T,
-    )
+    )]).T
 
 
 def solution(mesh):

time: 47.4 us -> 35.5 us (0.75)
  local copies, waits for them, and re-layouts: 9.1 us -> 0.6 us
  Pallas kernels: 37.9 us -> 34.7 us
    unnamed x18 -> x1, local copies, waits for them, and re-layouts: 8.43 us -> 0.6 us
    pallas_call x1, Pallas kernels: 37.9 us -> 34.7 us  [on_device(): pl.pallas_call(functools.partial(kernel, (n_group, n_page, n_tensor, slot...]
    pallas_call x1 -> x0, local copies, waits for them, and re-layouts: 0.67 us -> none  [on_device(): pl.pallas_call(functools.partial(kernel, (n_group, n_page, n_tensor, slot...]
where the time goes in v2:
time: 35.5 us; the launch traced here: 35.3 us
  Pallas kernels  34.7 us (98%)
  local copies, waits for them, and re-layouts  0.6 us (2%)
    pallas_call x1, Pallas kernels, on_device(): pl.pallas_call(functools.partial(kernel, (n_group, n_page, n_tensor, slot...  34.7 us

profile of v2, /device:TPU:1, one launch (start us, length us, event | category | flops | bytes accessed | tf_op | source)
XLA Modules:
  0.0 35.3 jit_solution(9237106949570637211)
XLA Ops:
  0.0 34.7 %shard_map.91 = bf16[16,32]{1,0:T(8,128)(2,1)S(1)} custom-call(bf16[32,2048]{1,0:T(8,128)(2,1)} %q_in.1, bf16[2048,256]{1,0:T(8,128)(2,1)} %bitcast.9, bf16[2048,256]{1,0:T(8,128)(2,1)} %bitcast.10, bf16[256,256]{1,0:T(8,128)(2,1)} %bitcast.12, bf16[256,256]{1,0:T(8,128)(2,1)} %bitcast.13, s32[2,2048]{1,0:T(2,128)} %bitcast.14, s32[32,2048]{1,0:T(8,128)} %tbl_in.1, ...), custom_call_target="tpu_custom_call" | custom-call | tf_op jit(solution)/shard_map/pallas_call | solution.py:441
  34.7 0.6 %copy.11 = bf16[32,16]{0,1:T(8,128)(2,1)} copy(bf16[32,16]{0,1:T(8,128)(2,1)S(1)} %bitcast.8) | data formatting | bytes 2048

commit v3 on v2

--- a/solution.py
+++ b/solution.py
@@ -14,6 +14,7 @@
 CORES = 2
 MESH = pl.DeviceIdType.MESH
 VERY_LOW = -1.0e30
+PVS = 2
 SCALE2 = HD**-0.5 * math.log2(math.e)
 NT = (((1,), (1,)), ((), ()))
 
@@ -230,17 +231,24 @@
 
     n_sheet = n_page * CORES
     place_b = z * CORES + core
-    greeted = [along_group(d) for d in range(1, n_group)]
-    for d in range(1, n_sheet):
-        if d % CORES == 0:
-            greeted.append(along_sheet(d))
-    greeted_cross = [d for d in range(1, n_sheet) if d % CORES]
-    greeted += [along_tensor(d) for d in range(1, n_tensor)]
     barrier = pltpu.get_barrier_semaphore()
-    for peer in greeted:
+
+    def other_core(place, d, count):
+        return lax.rem(place + d, count) * CORES + 1 - core
+
+    peers = []
+    for d in range(1, n_page):
+        hops = min(d, n_page - d)
+        peers.append((hops, along_page(d)))
+        peers.append((hops, {"group": y * CORES + 1 - core, "page": lax.rem(z + d, n_page)}))
+    for d in range(1, n_y):
+        hops = min(d, n_y - d)
+        peers.append((hops, along_y(d)))
+        peers.append((hops, {"group": other_core(y, d, n_y)}))
+    peers += [(min(d, n_tensor - d), along_tensor(d)) for d in range(1, n_tensor)]
+    peers.append((0, {"group": y * CORES + 1 - core}))
+    for _, peer in sorted(peers, key=lambda p: -p[0]):
         pl.semaphore_signal(barrier, inc=1, device_id=peer, device_id_type=MESH)
-    for d in greeted_cross:
-        pl.semaphore_signal(barrier, inc=1, device_id=along_sheet(d), device_id_type=MESH)
 
     def send(src, dst, peer, at):
         pltpu.make_async_remote_copy(
@@ -258,20 +266,24 @@
     def left(ref, at):
         pltpu.make_async_copy(ref, ref, send_sem.at[at]).wait()
 
-    for k in range(6):
+    for k in range(3):
         copies[k].wait()
-    for half in range(kv_heads):
+    build_bias(tbl, pm, lens, tgt, bias, gi, z, n_page, slots, new_dev)
+    for k in range(3, 6):
+        copies[k].wait()
+
+    def score(half):
         heads = range(half * share, (half + 1) * share)
         stacked = jnp.concatenate([q[:, h * HD : (h + 1) * HD] for h in heads], axis=0)
-        scores[half] = lax.dot_general(
+        s = lax.dot_general(
             stacked,
             key[:, half * HD : (half + 1) * HD],
             NT,
             preferred_element_type=jnp.float32,
         )
-    build_bias(tbl, pm, lens, tgt, bias, gi, z, n_page, slots, new_dev)
-    for k in range(6, 8):
-        copies[k].wait()
+        for h in range(share):
+            at = slice(h * seqs, (h + 1) * seqs)
+            scores[half, at, :] = s[at, :] * SCALE2 + bias[...]
 
     def far_first(count):
         return sorted(range(1, count), key=lambda d: -min(d, count - d))
@@ -279,9 +291,8 @@
     def soften(half):
         block = 16
         for b in range(rows // block):
-            s0 = b * block % seqs
             at = slice(b * block, (b + 1) * block)
-            s = scores[half, at, :] * SCALE2 + bias[s0 : s0 + block, :]
+            s = scores[half, at, :]
             top = jnp.max(s, axis=1, keepdims=True)
             probs[half, at, :] = jnp.exp2(s - top).astype(jnp.bfloat16)
             tops[half, at, :] = jnp.broadcast_to(top, (block, LANES))
@@ -290,7 +301,13 @@
         count, own_rows = part.shape[0], part.shape[1]
         v = value[:, half * HD : (half + 1) * HD]
         wide = jnp.concatenate([v, jnp.ones_like(v)], axis=1)
-        summed = jnp.dot(probs[half], wide, preferred_element_type=jnp.float32)
+        summed = jnp.concatenate(
+            [
+                jnp.dot(probs[half, i * rows // PVS : (i + 1) * rows // PVS, :], wide, preferred_element_type=jnp.float32)
+                for i in range(PVS)
+            ],
+            axis=0,
+        )
         shape = (own_rows, LANES)
         lane, row = lanes_of(shape), rows_of(shape)
         for k in range(count):
@@ -299,6 +316,9 @@
             sums = jnp.where(lane == row + own_rows, summed[at, HD:], 0.0)
             picked = jnp.where(lane == row, tops[half, at, :], sums)
             stat[k] = jnp.sum(picked, axis=0, keepdims=True)
+
+    def near_root(count):
+        return sorted(range(count), key=lambda k: min(k, count - k))
 
     def scatter(part, stat, got, gots, place, peer_of, at):
         count = part.shape[0]
@@ -318,10 +338,15 @@
         low = lanes_of((1, LANES)) < own_rows
         mids[...] = jnp.where(low, highest, pltpu.roll(total, own_rows, 1))
 
-    def spread(mid, mids, gotm, gotms, peer_of, at):
-        for d in far_first(gotm.shape[0] + 1):
-            send(mid, gotm.at[d - 1], peer_of(d), at)
-            send(mids, gotms.at[d - 1], peer_of(d), at + 1)
+    def spread(mid, mids, gotm, gotms, place, peer_at, at):
+        count = gotm.shape[0] + 1
+        for k in near_root(count):
+
+            @pl.when(place != k)
+            def _():
+                slot = lax.rem(k - place + count, count) - 1
+                send(mid, gotm.at[slot], peer_at(k), at)
+                send(mids, gotms.at[slot], peer_at(k), at + 1)
 
     def merge_spread(mid, mids, gotm, gotms, att, place, at):
         received(gotm, at)
@@ -332,29 +357,39 @@
         _, _, total_column, mixed = merge(stats, values, mid.shape[0])
         att[place] = (mixed / total_column).astype(jnp.bfloat16)
 
-    def gather(att, place, peer_of, at):
-        for d in far_first(att.shape[0]):
-            send(att.at[place], att.at[place], peer_of(d), at)
-
+    def gather(att, place, peer_at, at):
+        count = att.shape[0]
+        for k in near_root(count // CORES):
+            for c in (1, 0):
+                spot = k * CORES + c
+
+                @pl.when(place != spot)
+                def _():
+                    send(att.at[place], att.at[place], peer_at(k, c), at)
+
+    score(1)
+    soften(1)
+    for k in range(6, 8):
+        copies[k].wait()
+    weigh(1, part_b, stat_b)
+    pl.semaphore_wait(barrier, len(peers))
+    scatter(part_b, stat_b, got_b, gots_b, place_b, along_sheet, 2)
+    score(0)
     soften(0)
-    soften(1)
     weigh(0, part_a, stat_a)
-    pl.semaphore_wait(barrier, len(greeted) + len(greeted_cross))
     scatter(part_a, stat_a, got_a, gots_a, gi, along_group, 0)
-    weigh(1, part_b, stat_b)
-    scatter(part_b, stat_b, got_b, gots_b, place_b, along_sheet, 2)
+    merge_scattered(part_b, stat_b, got_b, gots_b, mid_b, mids_b, place_b, 2)
+    spread(mid_b, mids_b, gotm_b, gotms_b, y, lambda k: {"group": k * CORES + core}, 6)
     merge_scattered(part_a, stat_a, got_a, gots_a, mid_a, mids_a, gi, 0)
-    spread(mid_a, mids_a, gotm_a, gotms_a, along_page, 4)
-    merge_scattered(part_b, stat_b, got_b, gots_b, mid_b, mids_b, place_b, 2)
-    spread(mid_b, mids_b, gotm_b, gotms_b, along_y, 6)
+    spread(mid_a, mids_a, gotm_a, gotms_a, z, lambda k: {"page": k}, 4)
     left(got_a, 0)
     left(gots_a, 1)
     left(got_b, 2)
     left(gots_b, 3)
+    merge_spread(mid_b, mids_b, gotm_b, gotms_b, att_b, place_b, 6)
+    gather(att_b, place_b, lambda k, c: {"group": y * CORES + c, "page": k}, 9)
     merge_spread(mid_a, mids_a, gotm_a, gotms_a, att_a, gi, 4)
-    gather(att_a, gi, along_group, 8)
-    merge_spread(mid_b, mids_b, gotm_b, gotms_b, att_b, place_b, 6)
-    gather(att_b, place_b, along_sheet, 9)
+    gather(att_a, gi, lambda k, c: {"group": k * CORES + c}, 8)
     left(gotm_a, 4)
     left(gotms_a, 5)
     left(gotm_b, 6)

time: 35.5 us -> 34.3 us (0.966)
  Pallas kernels: 34.7 us -> 33.6 us
    pallas_call x1, Pallas kernels: 34.7 us -> 33.6 us  [on_device(): pl.pallas_call(functools.partial(kernel, (n_group, n_page, n_tensor, slot...]
where the time goes in v3:
time: 34.3 us; the launch traced here: 34.2 us
  Pallas kernels  33.6 us (98%)
  local copies, waits for them, and re-layouts  0.6 us (2%)
    pallas_call x1, Pallas kernels, on_device(): pl.pallas_call(functools.partial(kernel, (n_group, n_page, n_tensor, slot...  33.6 us

profile of v3, /device:TPU:1, one launch (start us, length us, event | category | flops | bytes accessed | tf_op | source)
XLA Modules:
  0.0 34.2 jit_solution(16896014438152203456)
XLA Ops:
  0.0 33.6 %shard_map.91 = bf16[16,32]{1,0:T(8,128)(2,1)S(1)} custom-call(bf16[32,2048]{1,0:T(8,128)(2,1)} %q_in.1, bf16[2048,256]{1,0:T(8,128)(2,1)} %bitcast.9, bf16[2048,256]{1,0:T(8,128)(2,1)} %bitcast.10, bf16[256,256]{1,0:T(8,128)(2,1)} %bitcast.12, bf16[256,256]{1,0:T(8,128)(2,1)} %bitcast.13, s32[2,2048]{1,0:T(2,128)} %bitcast.14, s32[32,2048]{1,0:T(8,128)} %tbl_in.1, ...), custom_call_target="tpu_custom_call" | custom-call | tf_op jit(solution)/shard_map/pallas_call | solution.py:476
  33.6 0.6 %copy.11 = bf16[32,16]{0,1:T(8,128)(2,1)} copy(bf16[32,16]{0,1:T(8,128)(2,1)S(1)} %bitcast.8) | data formatting | bytes 2048

commit v4 on v3

--- a/solution.py
+++ b/solution.py
@@ -320,12 +320,17 @@
     def near_root(count):
         return sorted(range(count), key=lambda k: min(k, count - k))
 
-    def scatter(part, stat, got, gots, place, peer_of, at):
+    def scatter(part, stat, got, gots, place, peer_at, at):
         count = part.shape[0]
-        for d in far_first(count):
-            owner = lax.rem(place + d, count)
-            send(part.at[owner], got.at[d - 1], peer_of(d), at)
-            send(stat.at[owner], gots.at[d - 1], peer_of(d), at + 1)
+        for k in reversed(near_root(count // CORES)):
+            for c in range(CORES):
+                spot = k * CORES + c
+
+                @pl.when(place != spot)
+                def _():
+                    slot = lax.rem(spot - place + count, count) - 1
+                    send(part.at[spot], got.at[slot], peer_at(k, c), at)
+                    send(stat.at[spot], gots.at[slot], peer_at(k, c), at + 1)
 
     def merge_scattered(part, stat, got, gots, mid, mids, place, at):
         count, own_rows = part.shape[0], part.shape[1]
@@ -373,11 +378,11 @@
         copies[k].wait()
     weigh(1, part_b, stat_b)
     pl.semaphore_wait(barrier, len(peers))
-    scatter(part_b, stat_b, got_b, gots_b, place_b, along_sheet, 2)
+    scatter(part_b, stat_b, got_b, gots_b, place_b, lambda k, c: {"group": y * CORES + c, "page": k}, 2)
     score(0)
     soften(0)
     weigh(0, part_a, stat_a)
-    scatter(part_a, stat_a, got_a, gots_a, gi, along_group, 0)
+    scatter(part_a, stat_a, got_a, gots_a, gi, lambda k, c: {"group": k * CORES + c}, 0)
     merge_scattered(part_b, stat_b, got_b, gots_b, mid_b, mids_b, place_b, 2)
     spread(mid_b, mids_b, gotm_b, gotms_b, y, lambda k: {"group": k * CORES + core}, 6)
     merge_scattered(part_a, stat_a, got_a, gots_a, mid_a, mids_a, gi, 0)

time: 34.3 us -> 34.3 us (level)
  no operation moved by 1% of the time
where the time goes in v4:
time: 34.3 us; the launch traced here: 34.1 us
  Pallas kernels  33.5 us (98%)
  local copies, waits for them, and re-layouts  0.6 us (2%)
    pallas_call x1, Pallas kernels, on_device(): pl.pallas_call(functools.partial(kernel, (n_group, n_page, n_tensor, slot...  33.5 us

profile of v4, /device:TPU:1, one launch (start us, length us, event | category | flops | bytes accessed | tf_op | source)
XLA Modules:
  0.0 34.1 jit_solution(5423847587405832818)
XLA Ops:
  0.0 33.5 %shard_map.91 = bf16[16,32]{1,0:T(8,128)(2,1)S(1)} custom-call(bf16[32,2048]{1,0:T(8,128)(2,1)} %q_in.1, bf16[2048,256]{1,0:T(8,128)(2,1)} %bitcast.9, bf16[2048,256]{1,0:T(8,128)(2,1)} %bitcast.10, bf16[256,256]{1,0:T(8,128)(2,1)} %bitcast.12, bf16[256,256]{1,0:T(8,128)(2,1)} %bitcast.13, s32[2,2048]{1,0:T(2,128)} %bitcast.14, s32[32,2048]{1,0:T(8,128)} %tbl_in.1, ...), custom_call_target="tpu_custom_call" | custom-call | tf_op jit(solution)/shard_map/pallas_call | solution.py:481
  33.6 0.6 %copy.11 = bf16[32,16]{0,1:T(8,128)(2,1)} copy(bf16[32,16]{0,1:T(8,128)(2,1)S(1)} %bitcast.8) | data formatting | bytes 2048

commit v5 on v4

--- a/solution.py
+++ b/solution.py
@@ -402,14 +402,17 @@
     others_a = att_a.at[pl.ds(0, n_group - 1)]
     others_b = att_b.at[pl.ds(0, n_sheet - 1)]
     copies[8].wait()
+
+    def project(att, first):
+        flat = att[...].reshape(rows, HD)
+        features = jnp.concatenate([flat[h * seqs : (h + 1) * seqs] for h in range(share)], axis=1)
+        block = weight[:, first * HD : (first + share) * HD]
+        return lax.dot_general(block, features, NT, preferred_element_type=jnp.float32)
+
+    received(others_b, 9)
+    last_out[...] = project(att_b, share)
     received(others_a, 8)
-    received(others_b, 9)
-    pieces = []
-    for att in (att_a, att_b):
-        flat = att[...].reshape(rows, HD)
-        pieces += [flat[h * seqs : (h + 1) * seqs] for h in range(share)]
-    features = jnp.concatenate(pieces, axis=1)
-    last_out[...] = lax.dot_general(weight[...], features, NT, preferred_element_type=jnp.float32)
+    last_out[...] += project(att_a, 0)
     width = out_ref.shape[0]
 
     def block_of(d):

time: 34.3 us -> 34.2 us (level)
  no operation moved by 1% of the time
where the time goes in v5:
time: 34.2 us; the launch traced here: 34.1 us
  Pallas kernels  33.5 us (98%)
  local copies, waits for them, and re-layouts  0.6 us (2%)
    pallas_call x1, Pallas kernels, on_device(): pl.pallas_call(functools.partial(kernel, (n_group, n_page, n_tensor, slot...  33.5 us

profile of v5, /device:TPU:1, one launch (start us, length us, event | category | flops | bytes accessed | tf_op | source)
XLA Modules:
  0.0 34.1 jit_solution(262246641082240975)
XLA Ops:
  0.0 33.5 %shard_map.91 = bf16[16,32]{1,0:T(8,128)(2,1)S(1)} custom-call(bf16[32,2048]{1,0:T(8,128)(2,1)} %q_in.1, bf16[2048,256]{1,0:T(8,128)(2,1)} %bitcast.9, bf16[2048,256]{1,0:T(8,128)(2,1)} %bitcast.10, bf16[256,256]{1,0:T(8,128)(2,1)} %bitcast.12, bf16[256,256]{1,0:T(8,128)(2,1)} %bitcast.13, s32[2,2048]{1,0:T(2,128)} %bitcast.14, s32[32,2048]{1,0:T(8,128)} %tbl_in.1, ...), custom_call_target="tpu_custom_call" | custom-call | tf_op jit(solution)/shard_map/pallas_call | solution.py:484
  33.5 0.6 %copy.11 = bf16[32,16]{0,1:T(8,128)(2,1)} copy(bf16[32,16]{0,1:T(8,128)(2,1)S(1)} %bitcast.8) | data formatting | bytes 2048
